TPU v7x, 256 devices: a whole 4x4x8 slice. The times are simulated.
256 devices in a mesh: rep: 4 (over x), fsdp: 32 (over y, z), tp: 2 (over core).
Axes of the slice: x: 4, y: 4, z: 8, core: 2. Of those that a mesh axis runs over, the one named last changes fastest.
Arguments:
- saved_inputs: bfloat16 [2, 32768, 768], P(None, ('rep', 'fsdp')), may hold values from -24 to 24
- out_cotangent: float32 [32768, 768], P(('rep', 'fsdp')), may hold values from -1.75 to 1.75
- gate_weight: bfloat16 [2, 768, 4480], P(None, 'fsdp', 'tp'), may hold values from -0.21875 to 0.21875
- up_weight: bfloat16 [2, 768, 4480], P(None, 'fsdp', 'tp'), may hold values from -0.21875 to 0.21875
- down_weight: bfloat16 [2, 768, 4480], P(None, 'fsdp', 'tp'), may hold values from -0.09375 to 0.09375
- norm_gain: bfloat16 [2, 768], P(None, 'fsdp'), may hold values from 0.5 to 1.5
- gate_accum: float32 [2, 768, 4480], P(None, 'fsdp', 'tp'), may hold values from -12 to 12
- up_accum: float32 [2, 768, 4480], P(None, 'fsdp', 'tp'), may hold values from -12 to 12
- down_accum: float32 [2, 768, 4480], P(None, 'fsdp', 'tp'), may hold values from -12 to 12
- gain_accum: float32 [2, 768], P(None, 'fsdp'), may hold values from -12 to 12
Outputs:
- input_cotangent: float32 [32768, 768], P(('rep', 'fsdp'))
- gate_grad: float32 [2, 768, 4480], P(None, 'fsdp', 'tp')
- up_grad: float32 [2, 768, 4480], P(None, 'fsdp', 'tp')
- down_grad: float32 [2, 768, 4480], P(None, 'fsdp', 'tp')
- gain_grad: float32 [2, 768], P(None, 'fsdp')
All inputs are finite; a program needn't handle non-finite values.
Results may differ from a plain program's by a relative error of at most 0.0025.
Values may be sent and summed in bfloat16 or wider, within the bound.
No kernel may reach another device: no remote copies, remote signals or barrier semaphores. Data moves between devices by JAX's collectives and lax.ppermute only.
A program may use at most 192 MiB of HBM per device.

v0:
```python
import jax
import jax.numpy as jnp
from jax import lax
from jax.sharding import PartitionSpec as P

epsilon = 1e-06


def as_sent(value):

    def short(part):
        return part.astype(jnp.bfloat16) if part.dtype == jnp.float32 else part

    return jax.tree.map(short, value)


def total_of_pieces(value, axis):
    return lax.all_gather(value, axis).sum(0)


def scattered(product, width, axis):
    everything = product(jnp.int32(0), lax.axis_size(axis) * width)
    own = lax.psum_scatter(everything, axis, scatter_dimension=0, tiled=True)
    return own


def fetch_layer(weight_stacks, layer_index):
    pieces = tuple(
        (
            lax.dynamic_index_in_dim(weight_stack, layer_index, 0, keepdims=False)
            for weight_stack in weight_stacks
        )
    )
    return (
        lax.all_gather(as_sent(pieces[0]), "fsdp", axis=0, tiled=True),
        lax.all_gather(as_sent(pieces[1]), "fsdp", axis=0, tiled=True),
        lax.all_gather(as_sent(pieces[2]), "fsdp", axis=0, tiled=True),
        lax.all_gather(as_sent(pieces[3]), "fsdp", axis=0, tiled=True),
    )


def layer_backward(saved_x, cotangent, weights):
    gate_full, up_full, down_full, gain_full = weights
    feature_count = saved_x.shape[1]
    inputs = saved_x.astype(jnp.float32)
    tok_scale = lax.rsqrt(jnp.mean(inputs * inputs, axis=1, keepdims=True) + epsilon)
    whitened = inputs * tok_scale
    gain_vec = gain_full.astype(jnp.float32)
    normed = (whitened * gain_vec).astype(jnp.bfloat16)
    gate_pre = jnp.dot(normed, gate_full, preferred_element_type=jnp.float32)
    up_pre = jnp.dot(normed, up_full, preferred_element_type=jnp.float32)
    sigmoid_gate = jax.nn.sigmoid(gate_pre)
    active = gate_pre * sigmoid_gate
    hidden = (active * up_pre).astype(jnp.bfloat16)
    upstream = cotangent.astype(jnp.bfloat16)
    grad_hidden = jnp.dot(upstream, down_full, preferred_element_type=jnp.float32)
    grad_gate = (
        grad_hidden * up_pre * (sigmoid_gate * (1.0 + gate_pre * (1.0 - sigmoid_gate)))
    ).astype(jnp.bfloat16)
    grad_up = (grad_hidden * active).astype(jnp.bfloat16)
    contract_cols = (((1,), (1,)), ((), ()))
    partial_grad = lax.dot_general(
        grad_gate, gate_full, contract_cols, preferred_element_type=jnp.float32
    )
    partial_grad = partial_grad + lax.dot_general(
        grad_up, up_full, contract_cols, preferred_element_type=jnp.float32
    )
    grad_normed = total_of_pieces(partial_grad, "tp")
    grad_white = grad_normed * gain_vec
    inner_mean = jnp.mean(grad_white * whitened, axis=1, keepdims=True)
    passed = cotangent + tok_scale * (grad_white - whitened * inner_mean)
    gain_total = jnp.sum(grad_normed * whitened, axis=0)
    contract_rows = (((0,), (0,)), ((), ()))

    def grad_term(row_start, row_count):
        rows_normed = lax.dynamic_slice_in_dim(normed, row_start, row_count, 1)
        rows_upstream = lax.dynamic_slice_in_dim(upstream, row_start, row_count, 1)
        gate_part = lax.dot_general(
            rows_normed, grad_gate, contract_rows, preferred_element_type=jnp.float32
        )
        up_part = lax.dot_general(
            rows_normed, grad_up, contract_rows, preferred_element_type=jnp.float32
        )
        down_part = lax.dot_general(
            rows_upstream, hidden, contract_rows, preferred_element_type=jnp.float32
        )
        gain_part = lax.dynamic_slice_in_dim(gain_total, row_start, row_count, 0)[:, None]
        return jnp.concatenate([gate_part, up_part, down_part, gain_part], axis=1)

    grad_shard = scattered(grad_term, feature_count // lax.axis_size("fsdp"), "fsdp")
    grad_shard = grad_shard
    return (passed, grad_shard)


def body(
    saved_inputs,
    out_cotangent,
    gate_weight,
    up_weight,
    down_weight,
    norm_gain,
    gate_accum,
    up_accum,
    down_accum,
    gain_accum,
):
    layers = saved_inputs.shape[0]
    hidden_local = gate_weight.shape[2]
    weight_stacks = (gate_weight, up_weight, down_weight, norm_gain)

    def layer_step(carry, slices):
        cotangent, weights = carry
        saved_x, layer_index = slices
        upcoming = fetch_layer(weight_stacks, layer_index - 1)
        passed, grad_shard = layer_backward(saved_x, cotangent, weights)
        return ((passed, upcoming), grad_shard)

    current = fetch_layer(weight_stacks, layers - 1)
    indices = jnp.arange(1, layers, dtype=jnp.int32)
    (passed, lowest), upper_shards = lax.scan(
        layer_step, (out_cotangent, current), (saved_inputs[1:], indices), reverse=True
    )
    cotangent, first_shard = layer_backward(saved_inputs[0], passed, lowest)
    shards = jnp.concatenate([first_shard[None], upper_shards], axis=0)
    shards = lax.psum(shards, "rep")
    gate_grad = gate_accum + shards[:, :, :hidden_local]
    up_grad = up_accum + shards[:, :, hidden_local : 2 * hidden_local]
    down_grad = down_accum + shards[:, :, 2 * hidden_local : 3 * hidden_local]
    gain_grad = gain_accum + shards[:, :, 3 * hidden_local]
    return (cotangent, gate_grad, up_grad, down_grad, gain_grad)


def solution(mesh):
    return jax.shard_map(
        body,
        mesh=mesh,
        in_specs=(
            P(None, ("rep", "fsdp"), None),
            P(("rep", "fsdp"), None),
            P(None, "fsdp", "tp"),
            P(None, "fsdp", "tp"),
            P(None, "fsdp", "tp"),
            P(None, "fsdp"),
            P(None, "fsdp", "tp"),
            P(None, "fsdp", "tp"),
            P(None, "fsdp", "tp"),
            P(None, "fsdp"),
        ),
        out_specs=(
            P(("rep", "fsdp"), None),
            P(None, "fsdp", "tp"),
            P(None, "fsdp", "tp"),
            P(None, "fsdp", "tp"),
            P(None, "fsdp"),
        ),
        check_vma=False,
    )
```

profile of v0, /device:TPU:8, one launch (start us, length us, event | category | flops | bytes accessed | tf_op | source)
XLA Modules:
  0.0 1303.9 jit_solution(17717513750796125036)
XLA Ops:
  15.6 66.2 %all-reduce.5 = (bf16[768]{0:T(1024)(128)(2,1)S(1)}, bf16[768]{0:T(1024)(128)(2,1)S(1)}) all-reduce(bf16[768]{0:T(1024)(128)(2,1)S(1)} %dynamic-update-slice, bf16[768]{0:T(1024)(128)(2,1)S(1)} %dynamic-update-slice.1), channel_id=3, replica_groups=mesh['rep'=4,'fsdp'=32,'tp'=2] {'fsdp'}, use_global_device_ids=true, to_apply=%add | all-reduce | flops 1536 | bytes 6144
  83.0 10.2 all-gather.21.cloned.1.call-done
  96.8 76.8 %all-gather.23.cloned.1.call-done = bf16[1,768,2240]{2,1,0:T(8,128)(2,1)} async-done(((bf16[1,24,2240]{2,1,0:T(8,128)(2,1)}), bf16[1,768,2240]{2,1,0:T(8,128)(2,1)}) %all-gather.23.cloned.1.call-update) | async-done | bytes 3440656 | tf_op jit(solution)/shard_map/all_gather | solution.py:35
  173.5 5.0 fusion.12
  178.5 74.8 %all-gather.19.cloned.1.call-done = bf16[1,768,2240]{2,1,0:T(8,128)(2,1)} async-done(((bf16[1,24,2240]{2,1,0:T(8,128)(2,1)}), bf16[1,768,2240]{2,1,0:T(8,128)(2,1)}) %all-gather.19.cloned.1.call-update) | async-done | bytes 3440656 | tf_op jit(solution)/shard_map/all_gather | solution.py:37
  253.3 5.2 multiply_convert_fusion.4
  265.6 5.4 fusion.65
  271.0 4.1 fusion.67
  275.1 4.1 convolution_bitcast_fusion
  281.6 78.6 %all-gather.31.cloned.1.call-done = bf16[1,768,2240]{2,1,0:T(8,128)(2,1)} async-done(((bf16[1,24,2240]{2,1,0:T(8,128)(2,1)}), bf16[1,768,2240]{2,1,0:T(8,128)(2,1)}) %all-gather.31.cloned.1.call-update) | async-done | bytes 3440656 | tf_op jit(solution)/shard_map/while/body/eval_jaxpr/all_gather | solution.py:35
  360.1 5.0 fusion.2
  365.1 75.2 %all-gather.29.cloned.1.call-done = bf16[1,768,2240]{2,1,0:T(8,128)(2,1)} async-done(((bf16[1,24,2240]{2,1,0:T(8,128)(2,1)}), bf16[1,768,2240]{2,1,0:T(8,128)(2,1)}) %all-gather.29.cloned.1.call-update) | async-done | bytes 3440656 | tf_op jit(solution)/shard_map/while/body/eval_jaxpr/all_gather | solution.py:36
  440.3 3.7 fusion.6
  445.4 4.2 fusion.28
  449.6 70.4 %all-gather.27.cloned.1.call-done = bf16[1,768,2240]{2,1,0:T(8,128)(2,1)} async-done(((bf16[1,24,2240]{2,1,0:T(8,128)(2,1)}), bf16[1,768,2240]{2,1,0:T(8,128)(2,1)}) %all-gather.27.cloned.1.call-update) | async-done | bytes 3440656 | tf_op jit(solution)/shard_map/while/body/eval_jaxpr/all_gather | solution.py:37
  520.1 5.4 multiply_convert_fusion.2
  525.5 4.3 fusion.59
  533.9 3.9 fusion.61
  537.8 15.0 %pad_maximum_fusion.1 = f32[768,6721]{0,1:T(8,128)} fusion(f32[768,1]{0,1:T(1,128)S(1)} %broadcast_in_dim.29, f32[768,2240]{0,1:T(8,128)} %convolution_bitcast_fusion, f32[768,2240]{0,1:T(8,128)} %fusion.67, f32[768,2240]{0,1:T(8,128)} %fusion.65), kind=kLoop, calls=%fused_computation.1 | loop fusion | flops 15485184 | bytes 41293824 | tf_op jit(solution)/shard_map/while/body/eval_jaxpr/concatenate | solution.py:88
  554.8 15.0 %pad_maximum_fusion = f32[768,6721]{0,1:T(8,128)} fusion(f32[768,1]{0,1:T(1,128)S(1)} %broadcast_in_dim.27, f32[768,2240]{0,1:T(8,128)} %fusion.28, f32[768,2240]{0,1:T(8,128)} %fusion.61, f32[768,2240]{0,1:T(8,128)} %fusion.59), kind=kLoop, calls=%fused_computation | loop fusion | flops 15485184 | bytes 41293824 | tf_op jit(solution)/shard_map/concatenate | solution.py:88
  570.5 650.6 %all-reduce.11.cloned.1.call-done = (f32[768,6721]{0,1:T(8,128)}, f32[768,6721]{0,1:T(8,128)}) async-done(((f32[768,6721]{0,1:T(8,128)}, f32[768,6721]{0,1:T(8,128)}), (f32[768,6721]{0,1:T(8,128)}, f32[768,6721]{0,1:T(8,128)})) %all-reduce.11.cloned.1.call-update) | async-done | bytes 41293840
  1221.2 5.7 dynamic-slice_bitcast_fusion
  1226.8 5.8 dynamic-slice_bitcast_fusion.1
  1242.0 51.0 %all-reduce.9.cloned.1.call-done = f32[2,24,6721]{2,1,0:T(8,128)} async-done(((f32[2,24,6721]{2,1,0:T(8,128)}), f32[2,24,6721]{2,1,0:T(8,128)}) %all-reduce.9.cloned.1.call-update) | async-done | bytes 1290448 | tf_op jit(solution)/shard_map/psum | solution.py:125
  (88 shorter events, 42.6 us)
Async XLA Ops:
  7.2 86.1 %copy-start = (bf16[2,256,768]{2,1,0:T(8,128)(2,1)S(1)}, bf16[2,256,768]{2,1,0:T(8,128)(2,1)}, u32[]{:S(2)}) copy-start(bf16[2,256,768]{2,1,0:T(8,128)(2,1)} %param.10) | copy-start | bytes 2359300
  7.2 86.0 %all-gather.21.cloned.1.call-start = ((), (), s32[]{:S(2)}) async-start(), calls=%async_computation.2 | async-start | bytes 3649536 | tf_op jit(solution)/shard_map/all_gather | solution.py:36
  9.0 164.6 %all-gather.23.cloned.1.call-start = ((), (), s32[]{:S(2)}) async-start(), calls=%async_computation.3 | async-start | bytes 3649536 | tf_op jit(solution)/shard_map/all_gather | solution.py:35
  10.7 242.6 %all-gather.19.cloned.1.call-start = ((), (), s32[]{:S(2)}) async-start(), calls=%async_computation.1 | async-start | bytes 3649536 | tf_op jit(solution)/shard_map/all_gather | solution.py:37
  12.4 266.8 %all-gather.25.cloned.1.call-start = ((), (), s32[]{:S(2)}) async-start(), calls=%async_computation.4 | async-start | bytes 2359296 | tf_op jit(solution)/shard_map/while/body/eval_jaxpr/all_gather | solution.py:18
  253.3 5.2 copy-start.2
  258.5 1.4 copy-start.8
  258.5 2.8 copy-start.1
  263.4 96.8 %all-gather.31.cloned.1.call-start = ((), (), s32[]{:S(2)}) async-start(), calls=%async_computation.7 | async-start | bytes 3649536 | tf_op jit(solution)/shard_map/while/body/eval_jaxpr/all_gather | solution.py:35
  264.0 176.3 %all-gather.29.cloned.1.call-start = ((), (), s32[]{:S(2)}) async-start(), calls=%async_computation.6 | async-start | bytes 3649536 | tf_op jit(solution)/shard_map/while/body/eval_jaxpr/all_gather | solution.py:36
  264.6 255.5 %all-gather.27.cloned.1.call-start = ((), (), s32[]{:S(2)}) async-start(), calls=%async_computation.5 | async-start | bytes 3649536 | tf_op jit(solution)/shard_map/while/body/eval_jaxpr/all_gather | solution.py:37
  265.3 287.6 %all-gather.33.cloned.1.call-start = ((), (), s32[]{:S(2)}) async-start(), calls=%async_computation.8 | async-start | bytes 2359296 | tf_op jit(solution)/shard_map/all_gather | solution.py:18
  265.5 5.4 copy-start.9
  270.9 4.1 copy-start.5
  270.9 4.1 copy-start.11
  279.2 2.1 copy-start.12
  440.3 5.1 copy-start.6
  525.5 4.3 copy-start.3
  529.8 2.0 copy-start.4
  533.9 687.3 %all-reduce.11.cloned.1.call-start = ((), (), s32[]{:S(2)}) async-start(), calls=%async_computation.9 | async-start | bytes 82673664
  569.8 723.1 %all-reduce.9.cloned.1.call-start = ((), (), s32[]{:S(2)}) async-start(), calls=%async_computation | async-start | bytes 2605056 | tf_op jit(solution)/shard_map/psum | solution.py:125
  1240.8 53.0 %copy-start.15 = (f32[2,24]{1,0:T(2,128)S(1)}, f32[2,24]{1,0:T(2,128)}, u32[]{:S(2)}) copy-start(f32[2,24]{1,0:T(2,128)} %param.19) | copy-start | bytes 580
  1240.8 53.6 %copy-start.13 = (f32[2,24,2240]{2,1,0:T(8,128)S(1)}, f32[2,24,2240]{2,1,0:T(8,128)}, u32[]{:S(2)}) copy-start(f32[2,24,2240]{2,1,0:T(8,128)} %param.18) | copy-start | bytes 1290244
  1240.8 53.6 %copy-start.14 = (f32[2,24,2240]{2,1,0:T(8,128)S(1)}, f32[2,24,2240]{2,1,0:T(8,128)}, u32[]{:S(2)}) copy-start(f32[2,24,2240]{2,1,0:T(8,128)} %param.17) | copy-start | bytes 1290244
  (2 other events, 2.5 us)
Sparse Core Ops, SparseCore 0:
  11.2 82.0 all-gather.20
  96.4 77.0 all-gather.22
  176.1 77.1 all-gather.18
  263.5 13.1 all-gather.24
  279.7 80.3 all-gather.30
  363.2 77.1 all-gather.28
  442.9 77.1 all-gather.26
  534.0 13.1 all-gather.32
  569.9 651.1 all-reduce.10
  1241.0 51.9 all-reduce.8
where the time goes:
time: 1300 us
  waiting for transfers between devices  1090 us (84%)
  blocking collectives  66.2 us (5%)
  matrix products  60.3 us (5%)
  other arithmetic  42 us (3%)
  local copies, waits for them, and re-layouts  29.7 us (2%)
  between operations  15.7 us (1%)
    unnamed x11, waiting for transfers between devices  653 us
    all_gather x2, waiting for transfers between devices, fetch_layer(): lax.all_gather(as_sent(pieces[0]), 'fsdp', axis=0, tiled=True)  155 us
    all_gather x2, waiting for transfers between devices, fetch_layer(): lax.all_gather(as_sent(pieces[2]), 'fsdp', axis=0, tiled=True)  145 us
    all_gather x2, waiting for transfers between devices, fetch_layer(): lax.all_gather(as_sent(pieces[1]), 'fsdp', axis=0, tiled=True)  85.4 us
    unnamed x1, blocking collectives  66.2 us
    psum x1, waiting for transfers between devices, body(): shards = lax.psum(shards, 'rep')  51 us
    concatenate x2, other arithmetic, grad_term(): return jnp.concatenate([gate_part, up_part, down_part, gain_part], axis=1)  30 us
  transfers between devices with their start and end apart: 10, of which 8 were waited for; matrix products, arithmetic and copies ran while one was open for 5% of the time, Pallas kernels for 0%

commit v1 on v0

--- a/solution.py
+++ b/solution.py
@@ -1,9 +1,19 @@
+import functools
 import jax
 import jax.numpy as jnp
 from jax import lax
 from jax.sharding import PartitionSpec as P
+from jax.lax import all_to_all, axis_size
 
 epsilon = 1e-06
+
+
+def meet_samples_all(in_array, chip_axis):
+    m_next = jnp.concatenate([in_array for _ in range(axis_size(chip_axis))], 0)
+    return all_to_all(m_next, chip_axis, 0, 0, tiled=True)
+
+
+serve_space_by_axis = functools.partial(meet_samples_all, chip_axis="fsdp")
 
 
 def as_sent(value):
@@ -34,7 +44,7 @@
     return (
         lax.all_gather(as_sent(pieces[0]), "fsdp", axis=0, tiled=True),
         lax.all_gather(as_sent(pieces[1]), "fsdp", axis=0, tiled=True),
-        lax.all_gather(as_sent(pieces[2]), "fsdp", axis=0, tiled=True),
+        serve_space_by_axis(as_sent(pieces[2])),
         lax.all_gather(as_sent(pieces[3]), "fsdp", axis=0, tiled=True),
     )
 

time: 1300 us -> 1210 us (0.931)
  waiting for transfers between devices: 1090 us -> 889 us
  blocking collectives: 66.2 us -> 151 us
  starting transfers between devices: 0.58 us -> 19.3 us
    all_gather x2 -> x0, waiting for transfers between devices: 145 us -> none  [fetch_layer(): lax.all_gather(as_sent(pieces[2]), 'fsdp', axis=0, tiled=True)]
    unnamed x1, blocking collectives: 66.2 us -> 151 us
    all_gather x2, waiting for transfers between devices: 155 us -> 109 us  [fetch_layer(): lax.all_gather(as_sent(pieces[0]), 'fsdp', axis=0, tiled=True)]
    all_to_all x0 -> x2, starting transfers between devices: none -> 18.8 us  [meet_samples_all(): return all_to_all(m_next, chip_axis, 0, 0, tiled=True)]
    unnamed x11 -> x9, waiting for transfers between devices: 653 us -> 652 us
  transfers between devices with their start and end apart: 10 -> 10, of which waited for: 8 -> 5; matrix products, arithmetic and copies ran while one was open for 5% -> 6% of each run, Pallas kernels for 0% -> 0%
where the time goes in v1:
time: 1210 us
  waiting for transfers between devices  889 us (73%)
  blocking collectives  151 us (12%)
  matrix products  61.1 us (5%)
  other arithmetic  41.5 us (3%)
  local copies, waits for them, and re-layouts  36.2 us (3%)
  starting transfers between devices  19.3 us (2%)
  between operations  16 us (1%)
    unnamed x9, waiting for transfers between devices  652 us
    unnamed x1, blocking collectives  151 us
    all_gather x2, waiting for transfers between devices, fetch_layer(): lax.all_gather(as_sent(pieces[0]), 'fsdp', axis=0, tiled=True)  109 us
    all_gather x2, waiting for transfers between devices, fetch_layer(): lax.all_gather(as_sent(pieces[1]), 'fsdp', axis=0, tiled=True)  76.2 us
    psum x1, waiting for transfers between devices, body(): shards = lax.psum(shards, 'rep')  51.2 us
    concatenate x2, other arithmetic, grad_term(): return jnp.concatenate([gate_part, up_part, down_part, gain_part], axis=1)  30.2 us
  transfers between devices with their start and end apart: 10, of which 5 were waited for; matrix products, arithmetic and copies ran while one was open for 6% of the time, Pallas kernels for 0%

profile of v1, /device:TPU:8, one launch (start us, length us, event | category | flops | bytes accessed | tf_op | source)
XLA Modules:
  0.0 1213.3 jit_solution(959273399058549291)
XLA Ops:
  20.6 11.9 all-to-all-start
  34.4 150.6 %all-reduce.5 = (bf16[768]{0:T(1024)(128)(2,1)S(1)}, bf16[768]{0:T(1024)(128)(2,1)S(1)}) all-reduce(bf16[768]{0:T(1024)(128)(2,1)S(1)} %dynamic-update-slice, bf16[768]{0:T(1024)(128)(2,1)S(1)} %dynamic-update-slice.1), channel_id=2, replica_groups=mesh['rep'=4,'fsdp'=32,'tp'=2] {'fsdp'}, use_global_device_ids=true, to_apply=%add | all-reduce | flops 1536 | bytes 6144
  185.2 3.6 fusion.14
  188.8 24.1 %all-gather.17.cloned.1.call-done = bf16[1,768,2240]{2,1,0:T(8,128)(2,1)} async-done(((bf16[1,24,2240]{2,1,0:T(8,128)(2,1)}), bf16[1,768,2240]{2,1,0:T(8,128)(2,1)}) %all-gather.17.cloned.1.call-update) | async-done | bytes 3440656 | tf_op jit(solution)/shard_map/all_gather | solution.py:45
  212.9 4.9 fusion.10
  217.8 4.9 multiply_convert_fusion.4
  228.8 7.0 all-to-all-start.1
  236.1 5.5 fusion.62
  241.5 3.9 fusion.64
  245.4 4.2 convolution_bitcast_fusion
  252.0 85.2 %all-gather.23.cloned.1.call-done = bf16[1,768,2240]{2,1,0:T(8,128)(2,1)} async-done(((bf16[1,24,2240]{2,1,0:T(8,128)(2,1)}), bf16[1,768,2240]{2,1,0:T(8,128)(2,1)}) %all-gather.23.cloned.1.call-update) | async-done | bytes 3440656 | tf_op jit(solution)/shard_map/while/body/eval_jaxpr/all_gather | solution.py:45
  337.3 4.9 fusion.2
  342.2 76.2 %all-gather.21.cloned.1.call-done = bf16[1,768,2240]{2,1,0:T(8,128)(2,1)} async-done(((bf16[1,24,2240]{2,1,0:T(8,128)(2,1)}), bf16[1,768,2240]{2,1,0:T(8,128)(2,1)}) %all-gather.21.cloned.1.call-update) | async-done | bytes 3440656 | tf_op jit(solution)/shard_map/while/body/eval_jaxpr/all_gather | solution.py:46
  418.3 3.7 fusion.6
  423.5 4.2 fusion.24
  427.7 5.5 multiply_convert_fusion.2
  433.2 4.2 fusion.56
  441.6 5.2 fusion.58
  446.8 15.1 %pad_maximum_fusion.1 = f32[768,6721]{0,1:T(8,128)} fusion(f32[768,1]{0,1:T(1,128)S(1)} %broadcast_in_dim.29, f32[768,2240]{0,1:T(8,128)} %convolution_bitcast_fusion, f32[768,2240]{0,1:T(8,128)} %fusion.64, f32[768,2240]{0,1:T(8,128)} %fusion.62), kind=kLoop, calls=%fused_computation.1 | loop fusion | flops 15485184 | bytes 41293824 | tf_op jit(solution)/shard_map/while/body/eval_jaxpr/concatenate | solution.py:98
  463.9 15.1 %pad_maximum_fusion = f32[768,6721]{0,1:T(8,128)} fusion(f32[768,1]{0,1:T(1,128)S(1)} %broadcast_in_dim.27, f32[768,2240]{0,1:T(8,128)} %fusion.24, f32[768,2240]{0,1:T(8,128)} %fusion.58, f32[768,2240]{0,1:T(8,128)} %fusion.56), kind=kLoop, calls=%fused_computation | loop fusion | flops 15485184 | bytes 41293824 | tf_op jit(solution)/shard_map/concatenate | solution.py:98
  479.8 650.7 %all-reduce.11.cloned.1.call-done = (f32[768,6721]{0,1:T(8,128)}, f32[768,6721]{0,1:T(8,128)}) async-done(((f32[768,6721]{0,1:T(8,128)}, f32[768,6721]{0,1:T(8,128)}), (f32[768,6721]{0,1:T(8,128)}, f32[768,6721]{0,1:T(8,128)})) %all-reduce.11.cloned.1.call-update) | async-done | bytes 41293840
  1130.4 5.6 dynamic-slice_bitcast_fusion
  1136.1 5.7 dynamic-slice_bitcast_fusion.1
  1151.1 51.2 %all-reduce.9.cloned.1.call-done = f32[2,24,6721]{2,1,0:T(8,128)} async-done(((f32[2,24,6721]{2,1,0:T(8,128)}), f32[2,24,6721]{2,1,0:T(8,128)}) %all-reduce.9.cloned.1.call-update) | async-done | bytes 1290448 | tf_op jit(solution)/shard_map/psum | solution.py:135
  (130 shorter events, 44.2 us)
Async XLA Ops:
  7.2 9.3 copy-start
  7.2 178.0 %all-gather.15.cloned.1.call-start = ((), (), s32[]{:S(2)}) async-start(), calls=%async_computation.3 | async-start | bytes 3649536 | tf_op jit(solution)/shard_map/all_gather | solution.py:46
  8.9 204.0 %all-gather.17.cloned.1.call-start = ((), (), s32[]{:S(2)}) async-start(), calls=%async_computation.4 | async-start | bytes 3649536 | tf_op jit(solution)/shard_map/all_gather | solution.py:45
  20.6 12.0 copy-start.21
  20.6 13.3 %copy-start.19 = (bf16[2,24]{1,0:T(2,128)(2,1)S(1)}, bf16[2,24]{1,0:T(2,128)(2,1)}, u32[]{:S(2)}) copy-start(bf16[2,24]{1,0:T(2,128)(2,1)} %param.15) | copy-start | bytes 292
  20.6 164.3 %copy-start.1 = (bf16[2,256,768]{2,1,0:T(8,128)(2,1)S(1)}, bf16[2,256,768]{2,1,0:T(8,128)(2,1)}, u32[]{:S(2)}) copy-start(bf16[2,256,768]{2,1,0:T(8,128)(2,1)} %param.10) | copy-start | bytes 2359300
  20.6 197.2 %all-to-all-start = ((bf16[32,24,2240]{2,1,0:T(8,128)(2,1)}), bf16[32,24,2240]{2,1,0:T(8,128)(2,1)}, u32[]{:S(2)}, u32[]{:S(2)}) async-start(bf16[32,24,2240]{2,1,0:T(8,128)(2,1)} %bitcast.146), calls=%async_computation | async-start | bytes 7077888 | tf_op jit(solution)/shard_map/all_to_all | solution.py:13
  32.5 217.1 %all-gather.19.cloned.1.call-start = ((), (), s32[]{:S(2)}) async-start(), calls=%async_computation.5 | async-start | bytes 2359296 | tf_op jit(solution)/shard_map/while/body/eval_jaxpr/all_gather | solution.py:28
  217.8 5.0 copy-start.5
  227.7 109.6 %all-gather.23.cloned.1.call-start = ((), (), s32[]{:S(2)}) async-start(), calls=%async_computation.7 | async-start | bytes 3649536 | tf_op jit(solution)/shard_map/while/body/eval_jaxpr/all_gather | solution.py:45
  228.2 190.1 %all-gather.21.cloned.1.call-start = ((), (), s32[]{:S(2)}) async-start(), calls=%async_computation.6 | async-start | bytes 3649536 | tf_op jit(solution)/shard_map/while/body/eval_jaxpr/all_gather | solution.py:46
  228.8 198.9 %all-to-all-start.1 = ((bf16[32,24,2240]{2,1,0:T(8,128)(2,1)}), bf16[32,24,2240]{2,1,0:T(8,128)(2,1)}, u32[]{:S(2)}, u32[]{:S(2)}) async-start(bf16[32,24,2240]{2,1,0:T(8,128)(2,1)} %bitcast.147), calls=%async_computation.1 | async-start | bytes 7077888 | tf_op jit(solution)/shard_map/while/body/eval_jaxpr/all_to_all | solution.py:13
  235.8 226.1 %all-gather.25.cloned.1.call-start = ((), (), s32[]{:S(2)}) async-start(), calls=%async_computation.8 | async-start | bytes 2359296 | tf_op jit(solution)/shard_map/all_gather | solution.py:28
  236.0 5.5 copy-start.12
  241.5 3.9 copy-start.8
  241.5 3.9 copy-start.15
  418.3 5.1 copy-start.9
  433.2 5.4 copy-start.14
  433.2 4.2 copy-start.6
  441.5 688.9 %all-reduce.11.cloned.1.call-start = ((), (), s32[]{:S(2)}) async-start(), calls=%async_computation.9 | async-start | bytes 82673664
  479.1 723.3 %all-reduce.9.cloned.1.call-start = ((), (), s32[]{:S(2)}) async-start(), calls=%async_computation.2 | async-start | bytes 2605056 | tf_op jit(solution)/shard_map/psum | solution.py:135
  1147.6 55.6 %copy-start.20 = (f32[2,24]{1,0:T(2,128)S(1)}, f32[2,24]{1,0:T(2,128)}, u32[]{:S(2)}) copy-start(f32[2,24]{1,0:T(2,128)} %param.19) | copy-start | bytes 580
  1149.9 53.8 %copy-start.17 = (f32[2,24,2240]{2,1,0:T(8,128)S(1)}, f32[2,24,2240]{2,1,0:T(8,128)}, u32[]{:S(2)}) copy-start(f32[2,24,2240]{2,1,0:T(8,128)} %param.18) | copy-start | bytes 1290244
  1149.9 53.8 %copy-start.18 = (f32[2,24,2240]{2,1,0:T(8,128)S(1)}, f32[2,24,2240]{2,1,0:T(8,128)}, u32[]{:S(2)}) copy-start(f32[2,24,2240]{2,1,0:T(8,128)} %param.17) | copy-start | bytes 1290244
  (8 other events, 14.6 us)
Sparse Core Ops, SparseCore 0:
  11.2 120.4 all-gather.14
  134.9 78.0 all-gather.16
  227.8 13.1 all-gather.18
  244.0 93.1 all-gather.22
  340.3 78.0 all-gather.20
  441.7 13.1 all-gather.24
  479.2 651.2 all-reduce.10
  1150.1 52.1 all-reduce.8
